TPU v7x, 32 devices: a whole 2x2x4 slice. The times are simulated.
32 devices in a mesh: groups: 2 (over x), tensor: 16 (over z, y, core).
Axes of the slice: x: 2, y: 2, z: 4, core: 2. Of those that a mesh axis runs over, the one named last changes fastest.
Arguments:
- video_state: float32 [128, 4096], P(('groups', 'tensor')), parts along dimension 0, may hold values from -54 to 54
- audio_state: float32 [128, 2048], P(('groups', 'tensor')), parts along dimension 0, may hold values from -54 to 54
- video_modulation: float32 [12, 4096], P('groups'), parts along dimension 0, may hold values from -3 to 3
- audio_modulation: float32 [12, 2048], P('groups'), parts along dimension 0, may hold values from -3 to 3
- video_query: bfloat16 [4096, 2048], P(None, 'tensor'), may hold values from -0.09375 to 0.09375
- audio_keyval: bfloat16 [2048, 2, 2048], P(None, None, 'tensor'), may hold values from -0.125 to 0.125
- video_output: bfloat16 [2048, 4096], P('tensor'), may hold values from -0.125 to 0.125
- audio_query: bfloat16 [2048, 2048], P(None, 'tensor'), may hold values from -0.125 to 0.125
- video_keyval: bfloat16 [4096, 2, 2048], P(None, None, 'tensor'), may hold values from -0.09375 to 0.09375
- audio_output: bfloat16 [2048, 2048], P('tensor'), may hold values from -0.125 to 0.125
- video_expand: bfloat16 [4096, 16384], P(None, 'tensor'), may hold values from -0.09375 to 0.09375
- video_shrink: bfloat16 [16384, 4096], P('tensor'), may hold values from -0.046875 to 0.046875
- audio_expand: bfloat16 [2048, 8192], P(None, 'tensor'), may hold values from -0.125 to 0.125
- audio_shrink: bfloat16 [8192, 2048], P('tensor'), may hold values from -0.0625 to 0.0625
Outputs:
- video_next: float32 [128, 4096], P(('groups', 'tensor')), parts along dimension 0
- audio_next: float32 [128, 2048], P(('groups', 'tensor')), parts along dimension 0
There are 2 independent parts, one for each index of `groups`. A program takes and returns all parts, laid end to end along the dimension named above; an argument that names none is the same for every part. Nothing has to cross between parts.
All inputs are finite; a program needn't handle non-finite values.
Results may differ from a plain program's by a relative error of at most 0.0029.
Values may be sent and summed in bfloat16 or wider, within the bound.
A program may use at most 64 MiB of HBM per device.

v0:
```python
import jax
import jax.numpy as jnp
from jax import lax
from jax.sharding import PartitionSpec as P

HEAD_DIM = 64
epsilon = 1e-06


def partner(block, axis, distance):
    count = lax.axis_size(axis)
    route = []
    for low in range(count):
        high = low | 1 << distance
        if high != low and high < count:
            route += [(low, high), (high, low)]
    return lax.ppermute(block, axis, route)


def modulate(states, modulation, first):
    normed = states * lax.rsqrt(jnp.mean(states * states, axis=-1, keepdims=True) + epsilon)
    return (normed * (1.0 + modulation[first + 1]) + modulation[first]).astype(jnp.bfloat16)


def head_normalize(tensor):
    values = tensor.astype(jnp.float32)
    return (values * lax.rsqrt(jnp.mean(values * values, axis=-1, keepdims=True) + epsilon)).astype(
        jnp.bfloat16
    )


def softmax_weights(scores):
    expo = jnp.exp(scores)
    return (expo / jnp.sum(expo, axis=-1, keepdims=True)).astype(jnp.bfloat16)


def local_heads(queries, key_part, value_part):
    query_count, width = queries.shape
    source_count = key_part.shape[0]
    head_count = width // HEAD_DIM
    query_hat = head_normalize(queries.reshape(query_count, head_count, HEAD_DIM))
    key_hat = head_normalize(key_part.reshape(source_count, head_count, HEAD_DIM))
    scores = jnp.einsum(
        "qhd,khd->hqk", query_hat, key_hat, preferred_element_type=jnp.float32
    ) * HEAD_DIM ** (-0.5)
    weights = softmax_weights(scores)
    values = value_part.reshape(source_count, head_count, HEAD_DIM)
    mixed = jnp.einsum("hqk,khd->qhd", weights, values, preferred_element_type=jnp.float32)
    return mixed.astype(jnp.bfloat16).reshape(query_count, width)


def project_attend(query_rows, source_rows, query_weight, keyval_weight):
    width = query_weight.shape[1]
    queries = jnp.dot(query_rows, query_weight, preferred_element_type=jnp.float32).astype(
        jnp.bfloat16
    )
    flat_weight = keyval_weight.reshape(keyval_weight.shape[0], 2 * width)
    keyvals = jnp.dot(source_rows, flat_weight, preferred_element_type=jnp.float32).astype(
        jnp.bfloat16
    )
    key_part = keyvals[:, :width]
    value_part = keyvals[:, width:]
    if width >= HEAD_DIM:
        return local_heads(queries, key_part, value_part)
    query_float = queries.astype(jnp.float32)
    key_float = key_part.astype(jnp.float32)
    query_square = jnp.sum(query_float * query_float, axis=1, keepdims=True)
    key_square = jnp.sum(key_float * key_float, axis=1, keepdims=True)
    other_query, other_key = partner((query_square, key_square), "tensor", 0)
    query_hat = (query_float * lax.rsqrt((query_square + other_query) / HEAD_DIM + epsilon)).astype(
        jnp.bfloat16
    )
    key_hat = (key_float * lax.rsqrt((key_square + other_key) / HEAD_DIM + epsilon)).astype(
        jnp.bfloat16
    )
    partial_scores = jnp.einsum("qd,kd->qk", query_hat, key_hat, preferred_element_type=jnp.float32)
    other_scores = partner(partial_scores, "tensor", 0)
    scores = (partial_scores + other_scores) * HEAD_DIM ** (-0.5)
    weights = softmax_weights(scores)
    return jnp.dot(weights, value_part, preferred_element_type=jnp.float32).astype(jnp.bfloat16)


def output_rows(mixed, weight):
    return jnp.dot(mixed, weight, preferred_element_type=jnp.float32)


def feed_rows(inputs, expand, shrink):
    hidden = jnp.dot(inputs, expand, preferred_element_type=jnp.float32)
    hidden = jax.nn.gelu(hidden, approximate=True).astype(jnp.bfloat16)
    return jnp.dot(hidden, shrink, preferred_element_type=jnp.float32)


def on_device(
    video_state,
    audio_state,
    video_modulation,
    audio_modulation,
    video_query,
    audio_keyval,
    video_output,
    audio_query,
    video_keyval,
    audio_output,
    video_expand,
    video_shrink,
    audio_expand,
    audio_shrink,
):
    video_count = video_state.shape[0]
    audio_own = modulate(audio_state, audio_modulation, 0)
    video_whole = lax.all_gather(video_state, "tensor", axis=0, tiled=True)
    video_normed = modulate(video_whole, video_modulation, 0)
    audio_normed = lax.all_gather(audio_own, "tensor", axis=0, tiled=True)
    video_mixed = project_attend(video_normed, audio_normed, video_query, audio_keyval)
    audio_mixed = project_attend(audio_normed, video_normed, audio_query, video_keyval)
    audio_term = lax.psum_scatter(
        output_rows(audio_mixed, audio_output), "tensor", scatter_dimension=0, tiled=True
    )
    audio_mid = audio_state + audio_modulation[2] * audio_term
    audio_inner_own = modulate(audio_mid, audio_modulation, 3)
    partial_term = jnp.dot(video_mixed, video_output, preferred_element_type=jnp.float32)
    full_term = lax.psum(partial_term, "tensor")
    video_mid_whole = video_whole + video_modulation[2] * full_term
    video_inner = modulate(video_mid_whole, video_modulation, 3)
    first_row = lax.axis_index("tensor") * video_count
    video_mid = lax.dynamic_slice_in_dim(video_mid_whole, first_row, video_count, 0)
    audio_inner = lax.all_gather(audio_inner_own, "tensor", axis=0, tiled=True)
    video_feed = lax.psum_scatter(
        feed_rows(video_inner, video_expand, video_shrink),
        "tensor",
        scatter_dimension=0,
        tiled=True,
    )
    audio_feed = lax.psum_scatter(
        feed_rows(audio_inner, audio_expand, audio_shrink),
        "tensor",
        scatter_dimension=0,
        tiled=True,
    )
    video_next = video_mid + video_modulation[5] * video_feed
    audio_next = audio_mid + audio_modulation[5] * audio_feed
    return (video_next, audio_next)


def solution(mesh):
    placed = (
        P(("groups", "tensor"), None),
        P(("groups", "tensor"), None),
        P("groups", None),
        P("groups", None),
        P(None, "tensor"),
        P(None, None, "tensor"),
        P("tensor", None),
        P(None, "tensor"),
        P(None, None, "tensor"),
        P("tensor", None),
        P(None, "tensor"),
        P("tensor", None),
        P(None, "tensor"),
        P("tensor", None),
    )
    return jax.shard_map(
        on_device,
        mesh=mesh,
        in_specs=placed,
        out_specs=(P(("groups", "tensor"), None), P(("groups", "tensor"), None)),
        check_vma=False,
    )
```

profile of v0, /device:TPU:0, one launch (start us, length us, event | category | flops | bytes accessed | tf_op | source)
XLA Modules:
  0.0 302.8 jit_solution(14228679446785322309)
XLA Ops:
  8.0 1.8 fusion.80
  9.7 0.9 multiply_reduce_fusion.7
  10.6 0.8 fusion.54
  11.5 24.0 %all-gather.1 = bf16[16,4,2048]{2,1,0:T(4,128)(2,1)S(1)} all-gather(bf16[1,4,2048]{2,1,0:T(4,128)(2,1)S(1)} %fusion.54), channel_id=1, replica_groups=mesh['groups'=2,'tensor'=16] {'tensor'}, dimensions={0}, use_global_device_ids=true | all-gather | bytes 278528 | tf_op jit(solution)/shard_map/all_gather | solution.py:113
  35.5 1.3 fusion.9
  36.9 1.5 convolution_convert_fusion.2
  40.3 10.6 %all-gather.5.cloned.1.call-done = f32[16,4,4096]{2,1,0:T(4,128)} async-done(((f32[1,4,4096]{2,1,0:T(4,128)}), f32[16,4,4096]{2,1,0:T(4,128)}) %all-gather.5.cloned.1.call-update) | async-done | bytes 1048592 | tf_op jit(solution)/shard_map/all_gather | solution.py:111
  50.9 1.6 reshape.111
  52.7 2.1 fusion.5
  55.9 1.6 fusion.8
  58.1 0.9 convolution_convert_fusion
  59.0 2.1 fusion.84
  61.6 0.9 convolution_convert_fusion.1
  62.5 2.6 fusion.83
  66.4 93.9 %all-reduce.10.cloned.1.call-done = (f32[64,4096]{1,0:T(8,128)}, f32[64,2048]{1,0:T(8,128)}) async-done(((f32[64,4096]{1,0:T(8,128)}, f32[64,2048]{1,0:T(8,128)}), (f32[64,4096]{1,0:T(8,128)}, f32[64,2048]{1,0:T(8,128)})) %all-reduce.10.cloned.1.call-update) | async-done | bytes 1572880 | tf_op jit(solution)/shard_map/psum | solution.py:122
  160.3 1.0 multiply_reduce_fusion.6
  161.4 21.4 %all-gather.2 = bf16[16,4,2048]{2,1,0:T(4,128)(2,1)} all-gather(bf16[1,4,2048]{2,1,0:T(4,128)(2,1)S(1)} %fusion.55), channel_id=1, replica_groups=mesh['groups'=2,'tensor'=16] {'tensor'}, dimensions={0}, use_global_device_ids=true | all-gather | bytes 278528 | tf_op jit(solution)/shard_map/all_gather | solution.py:127
  182.8 1.0 reshape.115
  183.8 2.5 multiply_reduce_fusion
  186.4 3.4 %fusion.37 = f32[64,2048]{1,0:T(8,128)} fusion(bf16[512,2048]{1,0:T(8,128)(2,1)S(1)} %copy-done, bf16[64,2048]{1,0:T(8,128)(2,1)S(1)} %reshape.115, bf16[2048,512]{1,0:T(8,128)(2,1)} %param.26), kind=kOutput, calls=%fused_computation.49 | convolution fusion | flops 268730368 | bytes 4980736 | tf_op jit(solution)/shard_map/dot_general | solution.py:90
  189.8 9.9 %fusion.24 = f32[64,4096]{1,0:T(8,128)} fusion(bf16[1024,4096]{1,0:T(8,128)(2,1)} %param.25, bf16[4096,1024]{1,0:T(8,128)(2,1)} %param.24, f32[64,4096]{1,0:T(8,128)S(1)} %copy-done.1, f32[4096]{0:T(1024)S(1)} %bitcast.60, f32[4096]{0:T(1024)S(1)} %bitcast.61, f32[64]{0:T(128)S(1)} %add_rsqrt_fusion.5), kind=kOutput, calls=%fused_computation.35 | convolution fusion | flops 1075380224 | bytes 18907392 | tf_op jit(solution)/shard_map/dot_general | solution.py:90
  199.8 93.4 %all-reduce.8.cloned.1.call-done = (f32[64,4096]{1,0:T(8,128)}, f32[64,2048]{1,0:T(8,128)}) async-done(((f32[64,4096]{1,0:T(8,128)}, f32[64,2048]{1,0:T(8,128)}), (f32[64,4096]{1,0:T(8,128)}, f32[64,2048]{1,0:T(8,128)})) %all-reduce.8.cloned.1.call-update) | async-done | bytes 1572880
  293.2 1.5 fusion.44
  294.7 1.6 fusion.39
  (63 shorter events, 5.7 us)
Async XLA Ops:
  7.2 179.2 %copy-start = (bf16[512,2048]{1,0:T(8,128)(2,1)S(1)}, bf16[512,2048]{1,0:T(8,128)(2,1)}, u32[]{:S(2)}) copy-start(bf16[512,2048]{1,0:T(8,128)(2,1)} %param.27) | copy-start | bytes 6291460
  7.2 32.4 %copy-start.3 = (f32[6,4096]{1,0:T(8,128)S(1)}, f32[6,4096]{1,0:T(8,128)}, u32[]{:S(2)}) copy-start(f32[6,4096]{1,0:T(8,128)} %param.16) | copy-start | bytes 294916
  7.2 43.8 %all-gather.5.cloned.1.call-start = ((), (), s32[]{:S(2)}) async-start(), calls=%async_computation | async-start | bytes 1114112 | tf_op jit(solution)/shard_map/all_gather | solution.py:111
  7.9 152.4 %all-reduce.10.cloned.1.call-start = ((), (), s32[]{:S(2)}) async-start(), calls=%async_computation.2 | async-start | bytes 3145728 | tf_op jit(solution)/shard_map/psum | solution.py:122
  40.3 14.5 %copy-start.4 = (f32[1,4096]{1,0:T(1,128)}, f32[1,4096]{1,0:T(1,128)S(1)}, u32[]{:S(2)}) copy-start(f32[1,4096]{1,0:T(1,128)S(1)} %get-tuple-element.11) | copy-start | bytes 49156
  40.3 14.6 %copy-start.5 = (f32[1,4096]{1,0:T(1,128)}, f32[1,4096]{1,0:T(1,128)S(1)}, u32[]{:S(2)}) copy-start(f32[1,4096]{1,0:T(1,128)S(1)} %get-tuple-element.12) | copy-start | bytes 49156
  61.4 3.8 %copy-start.13 = (u32[32]{0:T(128)S(1)}, u32[32]{0:T(128)}, u32[]{:S(2)}) copy-start(u32[32]{0:T(128)} %constant.50) | copy-start | bytes 388
  61.4 99.0 %copy-start.2 = (f32[4,2048]{1,0:T(4,128)S(1)}, f32[4,2048]{1,0:T(4,128)}, u32[]{:S(2)}) copy-start(f32[4,2048]{1,0:T(4,128)} %param.15) | copy-start | bytes 98308
  61.4 98.9 %copy-start.12 = (f32[1,2048]{1,0:T(1,128)S(1)}, f32[1,2048]{1,0:T(1,128)}, u32[]{:S(2)}) copy-start(f32[1,2048]{1,0:T(1,128)} %get-tuple-element.17) | copy-start | bytes 24580
  61.5 99.8 %copy-start.10 = (f32[1,2048]{1,0:T(1,128)S(1)}, f32[1,2048]{1,0:T(1,128)}, u32[]{:S(2)}) copy-start(f32[1,2048]{1,0:T(1,128)} %get-tuple-element.20) | copy-start | bytes 24580
  61.6 99.8 %copy-start.11 = (f32[1,2048]{1,0:T(1,128)S(1)}, f32[1,2048]{1,0:T(1,128)}, u32[]{:S(2)}) copy-start(f32[1,2048]{1,0:T(1,128)} %get-tuple-element.21) | copy-start | bytes 24580
  65.1 228.1 %all-reduce.8.cloned.1.call-start = ((), (), s32[]{:S(2)}) async-start(), calls=%async_computation.1 | async-start | bytes 3145728
  186.3 3.4 %copy-start.1 = (f32[64,4096]{1,0:T(8,128)S(1)}, f32[64,4096]{1,0:T(8,128)}, u32[]{:S(2)}) copy-start(f32[64,4096]{1,0:T(8,128)} %get-tuple-element.9) | copy-start | bytes 3145732
  186.3 3.4 %copy-start.7 = (f32[1,4096]{1,0:T(1,128)S(1)}, f32[1,4096]{1,0:T(1,128)}, u32[]{:S(2)}) copy-start(f32[1,4096]{1,0:T(1,128)} %get-tuple-element.14) | copy-start | bytes 49156
  186.3 3.4 %copy-start.8 = (f32[1,4096]{1,0:T(1,128)S(1)}, f32[1,4096]{1,0:T(1,128)}, u32[]{:S(2)}) copy-start(f32[1,4096]{1,0:T(1,128)} %get-tuple-element.15) | copy-start | bytes 49156
  189.8 103.4 %copy-start.9 = (f32[1,2048]{1,0:T(1,128)S(1)}, f32[1,2048]{1,0:T(1,128)}, u32[]{:S(2)}) copy-start(f32[1,2048]{1,0:T(1,128)} %get-tuple-element.16) | copy-start | bytes 24580
  189.8 104.9 %copy-start.6 = (f32[1,4096]{1,0:T(1,128)S(1)}, f32[1,4096]{1,0:T(1,128)}, u32[]{:S(2)}) copy-start(f32[1,4096]{1,0:T(1,128)} %get-tuple-element.10) | copy-start | bytes 49156
Sparse Core Ops, SparseCore 0:
  10.2 40.7 all-gather.4
  65.2 95.0 all-reduce.9
  199.9 93.2 all-reduce.7
where the time goes:
time: 304 us; the launch traced here: 303 us
  waiting for transfers between devices  199 us (65%)
  blocking collectives  45.4 us (15%)
  matrix products  26.7 us (9%)
  between operations  14.8 us (5%)
  other arithmetic  12 us (4%)
  local copies, waits for them, and re-layouts  5.14 us (2%)
    unnamed x4, waiting for transfers between devices  94.1 us
    psum x1, waiting for transfers between devices, on_device(): full_term = lax.psum(partial_term, 'tensor')  93.9 us
    all_gather x1, blocking collectives, on_device(): audio_normed = lax.all_gather(audio_own, 'tensor', axis=0, tiled=True)  24 us
    all_gather x1, blocking collectives, on_device(): audio_inner = lax.all_gather(audio_inner_own, 'tensor', axis=0, tiled=True)  21.4 us
    dot_general x2, matrix products, feed_rows(): return jnp.dot(hidden, shrink, preferred_element_type=jnp.float32)  13.4 us
    all_gather x1, waiting for transfers between devices, on_device(): video_whole = lax.all_gather(video_state, 'tensor', axis=0, tiled=True)  10.6 us
  transfers between devices with their start and end apart: 3, of which 3 were waited for; matrix products, arithmetic and copies ran while one was open for 3% of the time, Pallas kernels for 0%

commit v1 on v0

--- a/solution.py
+++ b/solution.py
@@ -119,7 +119,11 @@
     audio_mid = audio_state + audio_modulation[2] * audio_term
     audio_inner_own = modulate(audio_mid, audio_modulation, 3)
     partial_term = jnp.dot(video_mixed, video_output, preferred_element_type=jnp.float32)
-    full_term = lax.psum(partial_term, "tensor")
+    full_term = partial_term
+    for hop in (1, 2, 4, 8):
+        full_term = full_term + lax.ppermute(
+            full_term, "tensor", [(dev, dev ^ hop) for dev in range(16)]
+        )
     video_mid_whole = video_whole + video_modulation[2] * full_term
     video_inner = modulate(video_mid_whole, video_modulation, 3)
     first_row = lax.axis_index("tensor") * video_count

time: 304 us -> 376 us (1.24)
  blocking collectives: 45.4 us -> 78.8 us
  waiting for transfers between devices: 199 us -> 226 us
  other arithmetic: 12 us -> 21.7 us
  starting transfers between devices: 0.12 us -> 4.17 us
    psum x1 -> x0, waiting for transfers between devices: 93.9 us -> none  [on_device(): full_term = lax.psum(partial_term, 'tensor')]
    unnamed x4 -> x5, waiting for transfers between devices: 94.1 us -> 188 us
    all_gather x1, blocking collectives: 21.4 us -> 54.8 us  [on_device(): audio_inner = lax.all_gather(audio_inner_own, 'tensor', axis=0, tiled=True)]
    ppermute x0 -> x4, waiting for transfers between devices: none -> 26.3 us  [on_device(): lax.ppermute(full_term, 'tensor', [(dev, dev ^ hop) for dev in range(16)])]
    add x0 -> x3, other arithmetic: none -> 7.96 us  [on_device(): full_term + lax.ppermute(full_term, 'tensor', [(dev, dev ^ hop) for dev i...]
    ppermute x0 -> x4, starting transfers between devices: none -> 4.05 us  [on_device(): lax.ppermute(full_term, 'tensor', [(dev, dev ^ hop) for dev in range(16)])]
  transfers between devices with their start and end apart: 3 -> 7, of which waited for: 3 -> 5; matrix products, arithmetic and copies ran while one was open for 3% -> 5% of each run, Pallas kernels for 0% -> 0%
where the time goes in v1:
time: 376 us; the launch traced here: 375 us
  waiting for transfers between devices  226 us (60%)
  blocking collectives  78.8 us (21%)
  matrix products  24.1 us (6%)
  other arithmetic  21.7 us (6%)
  between operations  14.7 us (4%)
  local copies, waits for them, and re-layouts  5.86 us (2%)
  starting transfers between devices  4.17 us (1%)
    unnamed x5, waiting for transfers between devices  188 us
    all_gather x1, blocking collectives, on_device(): audio_inner = lax.all_gather(audio_inner_own, 'tensor', axis=0, tiled=True)  54.8 us
    ppermute x4, waiting for transfers between devices, on_device(): lax.ppermute(full_term, 'tensor', [(dev, dev ^ hop) for dev in range(16)])  26.3 us
    all_gather x1, blocking collectives, on_device(): audio_normed = lax.all_gather(audio_own, 'tensor', axis=0, tiled=True)  24 us
    dot_general x2, matrix products, feed_rows(): return jnp.dot(hidden, shrink, preferred_element_type=jnp.float32)  13.6 us
    all_gather x1, waiting for transfers between devices, on_device(): video_whole = lax.all_gather(video_state, 'tensor', axis=0, tiled=True)  11.6 us
    add x3, other arithmetic, on_device(): full_term + lax.ppermute(full_term, 'tensor', [(dev, dev ^ hop) for dev i...  7.96 us
  transfers between devices with their start and end apart: 7, of which 5 were waited for; matrix products, arithmetic and copies ran while one was open for 5% of the time, Pallas kernels for 0%

profile of v1, /device:TPU:0, one launch (start us, length us, event | category | flops | bytes accessed | tf_op | source)
XLA Modules:
  0.0 375.1 jit_solution(5204745635491179834)
XLA Ops:
  8.0 1.7 fusion.80
  11.5 24.0 %all-gather.1 = bf16[16,4,2048]{2,1,0:T(4,128)(2,1)S(1)} all-gather(bf16[1,4,2048]{2,1,0:T(4,128)(2,1)S(1)} %fusion.54), channel_id=1, replica_groups=mesh['groups'=2,'tensor'=16] {'tensor'}, dimensions={0}, use_global_device_ids=true | all-gather | bytes 278528 | tf_op jit(solution)/shard_map/all_gather | solution.py:113
  35.5 1.5 convolution_convert_fusion.2
  39.4 11.6 %all-gather.5.cloned.1.call-done = f32[16,4,4096]{2,1,0:T(4,128)} async-done(((f32[1,4,4096]{2,1,0:T(4,128)}), f32[16,4,4096]{2,1,0:T(4,128)}) %all-gather.5.cloned.1.call-update) | async-done | bytes 1048592 | tf_op jit(solution)/shard_map/all_gather | solution.py:111
  50.9 1.6 reshape.111
  53.3 2.2 fusion.8
  58.5 2.6 fusion.83
  61.9 2.3 collective-permute-done
  64.2 2.7 add.183
  68.4 24.0 %collective-permute-done.1 = f32[64,4096]{1,0:T(8,128)} collective-permute-done((f32[64,4096]{1,0:T(8,128)}, f32[64,4096]{1,0:T(8,128)}, u32[]{:S(2)}, u32[]{:S(2)}) %collective-permute-start.1) | collective-permute-done | bytes 1048608 | tf_op jit(solution)/shard_map/ppermute | solution.py:124
  92.4 2.7 add.184
  96.0 2.1 fusion.84
  99.4 89.4 %all-reduce.7.cloned.1.call-done = f32[64,2048]{1,0:T(8,128)} async-done(((f32[64,2048]{1,0:T(8,128)}), f32[64,2048]{1,0:T(8,128)}) %all-reduce.7.cloned.1.call-update) | async-done | bytes 524304
  188.8 1.0 multiply_reduce_fusion.6
  189.8 2.7 add.185
  192.5 2.9 collective-permute-start.3
  195.5 54.8 %all-gather.2 = bf16[16,4,2048]{2,1,0:T(4,128)(2,1)} all-gather(bf16[1,4,2048]{2,1,0:T(4,128)(2,1)S(1)} %fusion.55), channel_id=1, replica_groups=mesh['groups'=2,'tensor'=16] {'tensor'}, dimensions={0}, use_global_device_ids=true | all-gather | bytes 278528 | tf_op jit(solution)/shard_map/all_gather | solution.py:131
  250.3 1.0 reshape.115
  251.3 3.3 fusion.37
  254.7 2.8 multiply_reduce_fusion
  257.6 10.3 %fusion.24 = f32[64,4096]{1,0:T(8,128)} fusion(bf16[1024,4096]{1,0:T(8,128)(2,1)} %param.25, bf16[4096,1024]{1,0:T(8,128)(2,1)} %param.24, f32[64,4096]{1,0:T(8,128)} %get-tuple-element.7, f32[4096]{0:T(1024)S(1)} %bitcast.60, f32[4096]{0:T(1024)S(1)} %bitcast.61, f32[64]{0:T(128)S(1)} %add_rsqrt_fusion.5), kind=kOutput, calls=%fused_computation.35 | convolution fusion | flops 1075380224 | bytes 18907392 | tf_op jit(solution)/shard_map/dot_general | solution.py:90
  267.8 97.7 %all-reduce.9.cloned.1.call-done = (f32[64,4096]{1,0:T(8,128)}, f32[64,2048]{1,0:T(8,128)}) async-done(((f32[64,4096]{1,0:T(8,128)}, f32[64,2048]{1,0:T(8,128)}), (f32[64,4096]{1,0:T(8,128)}, f32[64,2048]{1,0:T(8,128)})) %all-reduce.9.cloned.1.call-update) | async-done | bytes 1572880
  365.5 1.5 fusion.44
  367.0 1.6 fusion.39
  (84 shorter events, 12.5 us)
Async XLA Ops:
  7.2 244.1 %copy-start = (bf16[512,2048]{1,0:T(8,128)(2,1)S(1)}, bf16[512,2048]{1,0:T(8,128)(2,1)}, u32[]{:S(2)}) copy-start(bf16[512,2048]{1,0:T(8,128)(2,1)} %param.27) | copy-start | bytes 6291460
  7.2 31.5 %copy-start.3 = (f32[6,4096]{1,0:T(8,128)S(1)}, f32[6,4096]{1,0:T(8,128)}, u32[]{:S(2)}) copy-start(f32[6,4096]{1,0:T(8,128)} %param.16) | copy-start | bytes 294916
  7.2 43.7 %all-gather.5.cloned.1.call-start = ((), (), s32[]{:S(2)}) async-start(), calls=%async_computation | async-start | bytes 1114112 | tf_op jit(solution)/shard_map/all_gather | solution.py:111
  7.9 180.9 %all-reduce.7.cloned.1.call-start = ((), (), s32[]{:S(2)}) async-start(), calls=%async_computation.1 | async-start | bytes 1048576
  39.4 13.3 %copy-start.4 = (f32[1,4096]{1,0:T(1,128)}, f32[1,4096]{1,0:T(1,128)S(1)}, u32[]{:S(2)}) copy-start(f32[1,4096]{1,0:T(1,128)S(1)} %get-tuple-element.9) | copy-start | bytes 49156
  39.4 13.4 %copy-start.6 = (f32[1,4096]{1,0:T(1,128)}, f32[1,4096]{1,0:T(1,128)S(1)}, u32[]{:S(2)}) copy-start(f32[1,4096]{1,0:T(1,128)S(1)} %get-tuple-element.10) | copy-start | bytes 49156
  61.2 6.1 %copy-start.5 = (f32[1,4096]{1,0:T(1,128)S(1)}, f32[1,4096]{1,0:T(1,128)}, u32[]{:S(2)}) copy-start(f32[1,4096]{1,0:T(1,128)} %copy-done.4) | copy-start | bytes 49156
  61.2 6.1 %copy-start.7 = (f32[1,4096]{1,0:T(1,128)S(1)}, f32[1,4096]{1,0:T(1,128)}, u32[]{:S(2)}) copy-start(f32[1,4096]{1,0:T(1,128)} %copy-done.6) | copy-start | bytes 49156
  61.2 6.1 %copy-start.16 = (f32[64]{0:T(128)S(1)}, f32[64]{0:T(128)}, u32[]{:S(2)}) copy-start(f32[64]{0:T(128)} %copy-done.15) | copy-start | bytes 772
  61.2 3.0 collective-permute-start
  61.7 5.6 %copy-start.17 = (bf16[4096,2,128]{2,1,0:T(2,128)(2,1)S(1)}, bf16[4096,2,128]{2,1,0:T(2,128)(2,1)}, u32[]{:S(2)}) copy-start(bf16[4096,2,128]{2,1,0:T(2,128)(2,1)} %param.22) | copy-start | bytes 6291460
  66.8 25.6 %collective-permute-start.1 = (f32[64,4096]{1,0:T(8,128)}, f32[64,4096]{1,0:T(8,128)}, u32[]{:S(2)}, u32[]{:S(2)}) collective-permute-start(f32[64,4096]{1,0:T(8,128)} %add.183), channel_id=1, source_target_pairs={{0,2},{1,3},{2,0},{3,1},{4,6},{5,7},{6,4},{7,5},{8,10},{9,11},{10,... | collective-permute-start | bytes 3145736 | tf_op jit(solution)/shard_map/ppermute | solution.py:124
  68.3 29.8 %copy-start.18 = (u32[32]{0:T(128)S(1)}, u32[32]{0:T(128)}, u32[]{:S(2)}) copy-start(u32[32]{0:T(128)} %constant.50) | copy-start | bytes 388
  68.3 120.5 %copy-start.2 = (f32[4,2048]{1,0:T(4,128)S(1)}, f32[4,2048]{1,0:T(4,128)}, u32[]{:S(2)}) copy-start(f32[4,2048]{1,0:T(4,128)} %param.15) | copy-start | bytes 98308
  68.4 120.5 %copy-start.14 = (f32[1,2048]{1,0:T(1,128)S(1)}, f32[1,2048]{1,0:T(1,128)}, u32[]{:S(2)}) copy-start(f32[1,2048]{1,0:T(1,128)} %get-tuple-element.15) | copy-start | bytes 24580
  95.1 94.8 %collective-permute-start.2 = (f32[64,4096]{1,0:T(8,128)}, f32[64,4096]{1,0:T(8,128)}, u32[]{:S(2)}, u32[]{:S(2)}) collective-permute-start(f32[64,4096]{1,0:T(8,128)} %add.184), channel_id=1, source_target_pairs={{0,4},{1,5},{2,6},{3,7},{4,0},{5,1},{6,2},{7,3},{8,12},{9,13},{10,... | collective-permute-start | bytes 3145736 | tf_op jit(solution)/shard_map/ppermute | solution.py:124
  98.1 97.3 %copy-start.12 = (f32[1,2048]{1,0:T(1,128)S(1)}, f32[1,2048]{1,0:T(1,128)}, u32[]{:S(2)}) copy-start(f32[1,2048]{1,0:T(1,128)} %get-tuple-element.18) | copy-start | bytes 24580
  98.1 97.3 %copy-start.13 = (f32[1,2048]{1,0:T(1,128)S(1)}, f32[1,2048]{1,0:T(1,128)}, u32[]{:S(2)}) copy-start(f32[1,2048]{1,0:T(1,128)} %get-tuple-element.19) | copy-start | bytes 24580
  98.1 267.4 %all-reduce.9.cloned.1.call-start = ((), (), s32[]{:S(2)}) async-start(), calls=%async_computation.2 | async-start | bytes 3145728
  192.5 62.2 %collective-permute-start.3 = (f32[64,4096]{1,0:T(8,128)}, f32[64,4096]{1,0:T(8,128)}, u32[]{:S(2)}, u32[]{:S(2)}) collective-permute-start(f32[64,4096]{1,0:T(8,128)} %add.185), channel_id=1, source_target_pairs={{0,8},{1,9},{2,10},{3,11},{4,12},{5,13},{6,14},{7,15},{8,0},{9,1},... | collective-permute-start | bytes 3145736 | tf_op jit(solution)/shard_map/ppermute | solution.py:124
  254.7 2.9 copy-start.9
  254.7 2.9 copy-start.10
  257.5 108.0 %copy-start.11 = (f32[1,2048]{1,0:T(1,128)S(1)}, f32[1,2048]{1,0:T(1,128)}, u32[]{:S(2)}) copy-start(f32[1,2048]{1,0:T(1,128)} %get-tuple-element.14) | copy-start | bytes 24580
  257.5 109.4 %copy-start.8 = (f32[1,4096]{1,0:T(1,128)S(1)}, f32[1,4096]{1,0:T(1,128)}, u32[]{:S(2)}) copy-start(f32[1,4096]{1,0:T(1,128)} %get-tuple-element.8) | copy-start | bytes 49156
  (2 other events, 3.4 us)
Sparse Core Ops, SparseCore 0:
  10.2 40.7 all-gather.4
  98.2 90.5 all-reduce.6
  267.9 97.5 all-reduce.8
